TPU v7x, 256 devices: a 4x2x16 block of a 4x16x16 slice. The times are simulated.
256 devices in a mesh: rep: 2 (over y), grp: 16 (over z), tp: 4 (over x), sub: 2 (over core).
Axes of the slice: x: 4, y: 2, z: 16, core: 2. Of those that a mesh axis runs over, the one named last changes fastest.
The devices are a block of a 4x16x16 slice.
Arguments:
- new_q: bfloat16 [16384, 8192], P(('rep', 'grp', 'sub'), 'tp'), parts along dimension 0
- new_kv: bfloat16 [2, 16384, 1024], P(None, ('rep', 'grp', 'sub'), 'tp'), parts along dimension 1
- hist_kv: bfloat16 [2, 32, 16, 1, 128, 1024], P(None, ('rep', 'grp'), None, None, 'sub', 'tp'), parts along dimension 1, may hold values from -6 to 6
- page_place: int32 [32, 16], P(('rep', 'grp')), parts along dimension 0, may hold values from 0 to 15, each once within a row
- hist_len: int32 [32], P(('rep', 'grp')), parts along dimension 0, may hold values from 1 to 2048, 16384 in all
- new_len: int32 [32], P(('rep', 'grp')), parts along dimension 0, may hold values from 128 to 512, as said below
- dec_q: bfloat16 [512, 8192], P(('rep', 'grp', 'sub'), 'tp'), parts along dimension 0
- dec_cache: bfloat16 [2, 512, 512, 1024], P(None, ('rep', 'grp', 'sub'), None, 'tp'), parts along dimension 1
- dec_len: int32 [512], P(('rep', 'grp', 'sub')), parts along dimension 0, may hold values from 64 to 512, as said below
Outputs:
- prefill_out: bfloat16 [16384, 8192], P(('rep', 'grp', 'sub'), 'tp'), parts along dimension 0
- decode_out: bfloat16 [512, 8192], P(('rep', 'grp', 'sub'), 'tp'), parts along dimension 0
There are 2 independent parts, one for each index of `rep`. A program takes and returns all parts, laid end to end along the dimension named above; each array names one. Nothing has to cross between parts.
Inputs may be any that keep to these rules, and one draw needn't show every extreme that they name: `page_place`: each row is an ordering of the slots 0 to 15: each owner holds exactly 1 pages of every conversation. `hist_len`: some conversation has exactly 2048. `new_len`: some conversation has exactly 512. `dec_len`: some request has exactly 512.
All inputs are finite; a program needn't handle non-finite values. No bound on the sum of `hist_len` on one device may be relied on, other than what follows from the above.
Results may differ from a plain program's by a relative error of at most 0.008.
Values may be sent and summed in bfloat16 or wider, within the bound.
A program may use at most 128 MiB of HBM per device.

v0:
```python
import math

import jax
import jax.numpy as jnp
from jax import lax
from jax.sharding import PartitionSpec as P

HQ = 64
KVH = 8
HD = 128
PAGE = 128


NEG = -1e30


def from_behind(block, axis, distance):
    devices = range(lax.axis_size(axis))
    route = [(i - distance, i) for i in devices if i - distance in devices]
    return lax.ppermute(block, axis, route)


def copy_for_each(shard, axis):
    devices = lax.axis_size(axis)
    return lax.all_to_all(
        jnp.broadcast_to(shard[None], (devices, *shard.shape)), axis, 0, 0, tiled=True
    )


def in_order(pieces, dim):
    dims = list(pieces.shape[1:])
    dims[dim] *= pieces.shape[0]
    return jnp.moveaxis(pieces, 0, dim).reshape(dims)


def collect(shard, axis, dim):
    pieces = copy_for_each(shard, axis)
    return in_order(pieces, dim)


def block_update(state, queries, keys, values, allowed, scale):
    top_old, total_old, acc_old = state
    scores = jnp.einsum("qkgd,skd->kgqs", queries, keys, preferred_element_type=jnp.float32) * scale
    scores = jnp.where(allowed[None, None], scores, NEG)
    top_new = jnp.maximum(top_old, jnp.max(scores, axis=-1))
    weights = jnp.exp(scores - top_new[..., None])
    factor = jnp.exp(top_old - top_new)
    total = total_old * factor + jnp.sum(weights, axis=-1)
    update = jnp.einsum(
        "kgqs,skd->kgqd", weights.astype(jnp.bfloat16), values, preferred_element_type=jnp.float32
    )
    return (top_new, total, acc_old * factor[..., None] + update)


def sweep(state, queries, keys, values, allowed, scale):
    count = keys.shape[0]
    width = math.gcd(count, 512)
    for begin in range(0, count, width):
        state = block_update(
            state,
            queries,
            keys[begin : begin + width],
            values[begin : begin + width],
            allowed[:, begin : begin + width],
            scale,
        )
    return state


def page_sweep(state, pages, start, page_of_slot, limit, queries, scale):
    slots = pages.shape[1]
    tokens = pages.shape[2]
    kv_local = pages.shape[3] // HD
    position = page_of_slot[:, None] * PAGE + start + jnp.arange(tokens, dtype=jnp.int32)[None, :]
    allowed = position.reshape(1, slots * tokens) < limit
    keys = pages[0].reshape(slots * tokens, kv_local, HD)
    values = pages[1].reshape(slots * tokens, kv_local, HD)
    return sweep(state, queries, keys, values, allowed, scale)


def local_decode(dec_q, dec_cache, dec_len, scale):
    requests = dec_q.shape[0]
    cached = dec_cache.shape[2]
    kv_local = dec_cache.shape[3] // HD
    group = HQ // KVH
    queries = dec_q.reshape(requests, kv_local, group, HD)
    keys = dec_cache[0].reshape(requests, cached, kv_local, HD)
    values = dec_cache[1].reshape(requests, cached, kv_local, HD)
    scores = (
        jnp.einsum("rkgd,rskd->rkgs", queries, keys, preferred_element_type=jnp.float32) * scale
    )
    allowed = (jnp.arange(cached, dtype=jnp.int32)[None, :] < dec_len[:, None])[:, None, None, :]
    scores = jnp.where(allowed, scores, NEG)
    top = jnp.max(scores, axis=-1, keepdims=True)
    weights = jnp.exp(scores - top)
    total = jnp.sum(weights, axis=-1)
    mixed = jnp.einsum(
        "rkgs,rskd->rkgd", weights.astype(jnp.bfloat16), values, preferred_element_type=jnp.float32
    )
    return (mixed / total[..., None]).reshape(requests, -1).astype(jnp.bfloat16)


def shards(new_q, new_kv, hist_kv, page_place, hist_len, new_len, dec_q, dec_cache, dec_len):
    scale = HD ** (-0.5)
    group = HQ // KVH
    rows = new_q.shape[0]
    kv_local = new_kv.shape[2] // HD
    queries = new_q.reshape(rows, kv_local, group, HD)
    decode_out = local_decode(dec_q, dec_cache, dec_len, scale)
    earlier = from_behind(new_kv, "sub", 1)
    query_pos = lax.axis_index("sub") * rows + jnp.arange(rows, dtype=jnp.int32)
    key_pos = jnp.concatenate([query_pos - rows, query_pos])
    both = jnp.concatenate([earlier, new_kv], axis=1)
    count = new_len[0]
    allowed = (
        (key_pos[None, :] >= 0)
        & (key_pos[None, :] <= query_pos[:, None])
        & (key_pos[None, :] < count)
    )
    state = sweep(
        (
            jnp.full((kv_local, group, rows), NEG, jnp.float32),
            jnp.zeros((kv_local, group, rows), jnp.float32),
            jnp.zeros((kv_local, group, rows, HD), jnp.float32),
        ),
        queries,
        both[0].reshape(2 * rows, kv_local, HD),
        both[1].reshape(2 * rows, kv_local, HD),
        allowed,
        scale,
    )
    place = page_place[0]
    slot_total = place.shape[0]
    slot_range = jnp.arange(slot_total, dtype=jnp.int32)
    match = place[None, :] == slot_range[:, None]
    page_of_slot = jnp.sum(jnp.where(match, slot_range[None, :], 0), axis=1)
    limit = hist_len[0]
    arrived = lax.all_to_all(hist_kv, "grp", split_axis=2, concat_axis=1, tiled=True)
    pages = arrived.reshape(
        2, arrived.shape[1] * arrived.shape[3], arrived.shape[4], arrived.shape[5]
    )
    whole = collect(pages, "sub", 2)
    state = page_sweep(state, whole, 0, page_of_slot, limit, queries, scale)
    top, total, acc = state
    mixed = jnp.transpose(acc / total[..., None], (2, 0, 1, 3)).reshape(rows, -1)
    prefill_out = jnp.where((query_pos < count)[:, None], mixed, 0.0).astype(jnp.bfloat16)
    return (prefill_out, decode_out)


def solution(mesh):
    in_specs = (
        P(("rep", "grp", "sub"), "tp"),
        P(None, ("rep", "grp", "sub"), "tp"),
        P(None, ("rep", "grp"), None, None, "sub", "tp"),
        P(("rep", "grp"), None),
        P(("rep", "grp")),
        P(("rep", "grp")),
        P(("rep", "grp", "sub"), "tp"),
        P(None, ("rep", "grp", "sub"), None, "tp"),
        P(("rep", "grp", "sub")),
    )
    out_specs = (P(("rep", "grp", "sub"), "tp"), P(("rep", "grp", "sub"), "tp"))
    return jax.shard_map(shards, mesh=mesh, in_specs=in_specs, out_specs=out_specs, check_vma=False)
```

profile of v0, /device:TPU:33, one launch (start us, length us, event | category | flops | bytes accessed | tf_op | source)
XLA Modules:
  0.0 136.8 jit_solution(12321260747631724067)
XLA Ops:
  0.6 2.3 %copy.94 = bf16[2,1,16,1,64,256]{5,4,3,1,0,2:T(8,128)(2,1)} copy(bf16[2,1,16,1,64,256]{5,4,3,2,1,0:T(8,128)(2,1)} %param.11) | data formatting | bytes 2097152 | tf_op args[2]
  2.9 24.5 %all-to-all-start = ((bf16[2,1,16,1,64,256]{5,4,3,1,0,2:T(8,128)(2,1)}), bf16[2,1,16,1,64,256]{5,4,3,1,0,2:T(8,128)(2,1)S(1)}, u32[]{:S(2)}, u32[]{:S(2)}) async-start(bf16[2,1,16,1,64,256]{5,4,3,1,0,2:T(8,128)(2,1)} %copy.94), calls=%async_computation | async-start | bytes 2097152 | tf_op jit(solution)/shard_map/all_to_all | solution.py:138
  27.5 1.1 copy.89
  28.5 1.3 collective-permute-start
  31.2 0.8 select_reduce_fusion
  32.1 4.5 %fusion.89 = (bf16[1,8,512,256]{3,2,1,0:T(8,128)(2,1)}, bf16[1,8,512,256]{3,2,1,0:T(8,128)(2,1)}) fusion(bf16[2,8,512,256]{3,2,1,0:T(8,128)(2,1)} %param.16), kind=kLoop, calls=%fused_computation.135 | loop fusion | bytes 8388608 | tf_op jit(solution)/shard_map/slice | solution.py:87
  36.6 2.9 %copy.161 = bf16[1,8,512,256]{2,3,1,0:T(8,128)(2,1)S(1)} copy(bf16[1,8,512,256]{3,2,1,0:T(8,128)(2,1)} %get-tuple-element.14) | data formatting | bytes 4194304
  39.5 3.9 %copy.162 = bf16[1,8,512,256]{2,3,1,0:T(8,128)(2,1)} copy(bf16[1,8,512,256]{3,2,1,0:T(8,128)(2,1)} %get-tuple-element.15) | data formatting | bytes 4194304
  44.8 2.3 %fusion.39 = bf16[1,8,16,128]{3,2,1,0:T(8,128)(2,1)S(1)} fusion(bf16[8,512,2,128]{1,3,2,0:T(8,128)(2,1)} %bitcast.260, f32[8,2,8,512]{3,2,1,0:T(8,128)S(1)} %get-tuple-element.42, f32[8,2,8]{2,1,0:T(2,128)S(1)} %get-tuple-element.41, f32[8,2,8]{2,1,0:T(2,128)S(1)} %fusion.59), kind=kOutput, calls=%fused_computation.54 | convolution fusion | flops 16941056 | bytes 2393088 | tf_op jit(solution)/shard_map/rkgs,rskd->rkgd/dot_general | solution.py:97
  47.7 1.4 %copy.163 = bf16[32,8,16,128]{3,2,1,0:T(8,128)(2,1)S(1)} copy(bf16[32,8,16,128]{3,1,2,0:T(8,128)(2,1)} %bitcast.265) | data formatting | bytes 2097152
  49.2 0.6 copy.208
  50.1 1.7 %pad_maximum_fusion = (bf16[1,512,256]{1,2,0:T(8,128)(2,1)}, bf16[1,512,256]{1,2,0:T(8,128)(2,1)S(1)}) fusion(bf16[2,256,256]{1,2,0:T(8,128)(2,1)S(1)} %copy.89, bf16[2,256,256]{1,2,0:T(8,128)(2,1)} %collective-permute-done), kind=kLoop, calls=%fused_computation.69 | loop fusion | flops 1048576 | bytes 1048576 | tf_op jit(solution)/shard_map/concatenate | solution.py:113
  51.8 4.9 %fusion.6 = (f32[2,8,256]{2,1,0:T(8,128)S(1)}, f32[2,512,256,8]{2,1,3,0:T(8,128)}) fusion(pred[256,512]{0,1:T(8,128)(4,1)S(1)} %and_and_fusion, bf16[512,2,128,1]{0,2,3,1:T(8,128)(2,1)S(1)} %bitcast.267, bf16[256,2,8,128]{3,2,1,0:T(8,128)(2,1)S(1)} %bitcast.248), kind=kOutput, calls=%fused_computation.20 | convolution fusion | flops 543158272 | bytes 9846784 | tf_op jit(solution)/shard_map/qkgd,skd->kgqs/dot_general | solution.py:43
  56.7 15.7 %all-to-all-done = bf16[2,1,16,1,64,256]{5,4,3,1,0,2:T(8,128)(2,1)S(1)} async-done(((bf16[2,1,16,1,64,256]{5,4,3,1,0,2:T(8,128)(2,1)}), bf16[2,1,16,1,64,256]{5,4,3,1,0,2:T(8,128)(2,1)S(1)}, u32[]{:S(2)}, u32[]{:S(2)}) %all-to-all-start) | async-done | bytes 1048608 | tf_op jit(solution)/shard_map/all_to_all | solution.py:138
  72.7 10.9 %all_to_all.14 = bf16[2,2,16,64,256]{4,3,2,1,0:T(8,128)(2,1)S(1)} all-to-all(bf16[2,2,16,64,256]{4,3,2,1,0:T(8,128)(2,1)S(1)} %broadcast_in_dim.143), channel_id=1, replica_groups=mesh['rep'=2,'grp'=16,'tp'=4,'sub'=2] {'sub'}, dimensions={0} | all-to-all | bytes 4194304 | tf_op jit(solution)/shard_map/all_to_all | solution.py:25
  84.0 0.7 copy.108
  84.7 1.0 slice.98
  85.7 0.8 slice.93
  88.1 5.4 %bitcast_reduce_fusion = (f32[2,8,256]{2,1,0:T(8,128)S(1)}, f32[2,512,256,8]{2,1,3,0:T(8,128)}) fusion(pred[512]{0:T(512)(128)(4,1)} %get-tuple-element.2, bf16[256,2,8,128]{3,2,1,0:T(8,128)(2,1)S(1)} %bitcast.249, bf16[512,2,128,1]{2,1,0,3:T(2,128)(2,1)S(1)} %bitcast.262), kind=kOutput, calls=%fused_computation.1 | convolution fusion | flops 543158272 | bytes 9716224 | tf_op jit(solution)/shard_map/qkgd,skd->kgqs/dot_general | solution.py:43
  93.6 4.7 %bitcast_reduce_fusion.1 = (f32[2,8,256]{2,1,0:T(8,128)S(1)}, f32[2,512,256,8]{2,1,3,0:T(8,128)}) fusion(pred[512]{0:T(512)(128)(4,1)S(1)} %copy-done.4, bf16[256,2,8,128]{3,2,1,0:T(8,128)(2,1)S(1)} %bitcast.250, bf16[512,2,128,1]{2,1,0,3:T(2,128)(2,1)S(1)} %bitcast.263), kind=kOutput, calls=%fused_computation.4 | convolution fusion | flops 543158272 | bytes 9716224 | tf_op jit(solution)/shard_map/qkgd,skd->kgqs/dot_general | solution.py:43
  98.3 1.5 %bitcast_reduce_fusion.2 = (f32[2,8,256]{2,1,0:T(8,128)S(1)}, f32[2,512,256,8]{2,1,3,0:T(8,128)S(1)}) fusion(pred[512]{0:T(512)(128)(4,1)S(1)} %copy-done.5, bf16[256,2,8,128]{3,2,1,0:T(8,128)(2,1)S(1)} %bitcast.251, bf16[512,2,128,1]{2,1,0,3:T(2,128)(2,1)S(1)} %bitcast.264), kind=kOutput, calls=%fused_computation.7 | convolution fusion | flops 543158272 | bytes 9716224 | tf_op jit(solution)/shard_map/qkgd,skd->kgqs/dot_general | solution.py:43
  99.8 1.5 %bitcast_reduce_fusion.3 = (f32[2,8,256]{2,1,0:T(8,128)S(1)}, f32[2,512,256,8]{2,1,3,0:T(8,128)S(1)}) fusion(pred[512]{0:T(512)(128)(4,1)S(1)} %copy-done.6, bf16[256,2,8,128]{3,2,1,0:T(8,128)(2,1)S(1)} %bitcast.252, bf16[512,2,128,1]{2,1,0,3:T(2,128)(2,1)S(1)} %bitcast.261), kind=kOutput, calls=%fused_computation.10 | convolution fusion | flops 543158272 | bytes 9716224 | tf_op jit(solution)/shard_map/qkgd,skd->kgqs/dot_general | solution.py:43
  101.4 3.5 %fusion.21 = f32[2,8,256,128]{2,3,1,0:T(8,128)} fusion(f32[2,512,256,8]{2,1,3,0:T(8,128)S(1)} %get-tuple-element.38, f32[2,8,256]{2,1,0:T(8,128)S(1)} %get-tuple-element.13, pred[512]{0:T(512)(128)(4,1)S(1)} %copy-done.6, bf16[512,2,128,1]{0,2,1,3:T(8,128)(2,1)S(1)} %reshape.290), kind=kOutput, calls=%fused_computation.32 | convolution fusion | flops 545259520 | bytes 10764800 | tf_op jit(solution)/shard_map/kgqs,skd->kgqd/dot_general | solution.py:49
  104.8 4.3 %fusion.7 = (f32[2,8,256]{2,1,0:T(8,128)S(1)}, f32[2,8,256]{2,1,0:T(8,128)S(1)}) fusion(f32[2,512,256,8]{2,1,3,0:T(8,128)S(1)} %get-tuple-element.38, f32[2,8,256]{2,1,0:T(8,128)S(1)} %get-tuple-element.13, pred[512]{0:T(512)(128)(4,1)S(1)} %copy-done.6, f32[2,8,256]{2,1,0:T(8,128)S(1)} %get-tuple-element.12, f32[2,512,256,8]{2,1,3,0:T(8,128)S(1)} %get-tuple-element.36, ...), kind=kLoop, calls=%fused_computation.21 | loop fusion | flops 16769024 | bytes 16843776 | tf_op jit(solution)/shard_map/reduce_sum | solution.py:48
  109.1 3.6 %fusion.19 = f32[2,8,256,128]{2,3,1,0:T(8,128)} fusion(f32[2,512,256,8]{2,1,3,0:T(8,128)S(1)} %get-tuple-element.36, f32[2,8,256]{2,1,0:T(8,128)S(1)} %get-tuple-element.12, pred[512]{0:T(512)(128)(4,1)S(1)} %copy-done.5, bf16[512,2,128,1]{0,2,1,3:T(8,128)(2,1)S(1)} %reshape.292), kind=kOutput, calls=%fused_computation.31 | convolution fusion | flops 545259520 | bytes 10764800 | tf_op jit(solution)/shard_map/kgqs,skd->kgqd/dot_general | solution.py:49
  114.3 5.7 %fusion.17 = f32[2,8,256,128]{2,3,1,0:T(8,128)S(1)} fusion(f32[2,512,256,8]{2,1,3,0:T(8,128)} %get-tuple-element.34, f32[2,8,256]{2,1,0:T(8,128)S(1)} %get-tuple-element.11, pred[512]{0:T(512)(128)(4,1)S(1)} %copy-done.4, bf16[512,2,128,1]{0,2,1,3:T(8,128)(2,1)S(1)} %reshape.294), kind=kOutput, calls=%fused_computation.30 | convolution fusion | flops 545259520 | bytes 10764800 | tf_op jit(solution)/shard_map/kgqs,skd->kgqd/dot_general | solution.py:49
  120.0 8.0 %fusion.11 = (f32[2,8,256]{2,1,0:T(8,128)S(1)}, f32[2,8,256]{2,1,0:T(8,128)S(1)}) fusion(f32[2,512,256,8]{2,1,3,0:T(8,128)} %get-tuple-element.34, f32[2,8,256]{2,1,0:T(8,128)S(1)} %get-tuple-element.11, pred[512]{0:T(512)(128)(4,1)S(1)} %copy-done.4, f32[2,8,256]{2,1,0:T(8,128)S(1)} %get-tuple-element.10, f32[2,512,256,8]{2,1,3,0:T(8,128)} %get-tuple-element.32, ...), kind=kLoop, calls=%fused_computation.25 | loop fusion | flops 16769024 | bytes 16843776 | tf_op jit(solution)/shard_map/reduce_sum | solution.py:48
  128.0 2.2 %fusion.15 = f32[2,8,256,128]{2,3,1,0:T(8,128)S(1)} fusion(f32[2,512,256,8]{2,1,3,0:T(8,128)S(1)} %bitcast.256, f32[2,8,256]{2,1,0:T(8,128)S(1)} %get-tuple-element.10, pred[512]{0:T(512)(128)(4,1)S(1)} %copy-done.3, bf16[512,2,128,1]{0,2,1,3:T(8,128)(2,1)S(1)} %reshape.296), kind=kOutput, calls=%fused_computation.29 | convolution fusion | flops 545259520 | bytes 10764800 | tf_op jit(solution)/shard_map/kgqs,skd->kgqd/dot_general | solution.py:49
  130.2 1.7 %fusion.4 = f32[2,8,256]{2,1,0:T(8,128)S(1)} fusion(f32[2,512,256,8]{2,1,3,0:T(8,128)S(1)} %bitcast.254, f32[2,8,256]{2,1,0:T(8,128)S(1)} %get-tuple-element.28, pred[256,512]{0,1:T(8,128)(4,1)S(1)} %and_and_fusion), kind=kLoop, calls=%fused_computation.18 | loop fusion | flops 8384512 | bytes 8552448 | tf_op jit(solution)/shard_map/reduce_sum | solution.py:48
  132.0 2.9 %fusion.30 = bf16[256,2,8,128]{0,3,2,1:T(8,128)(2,1)S(1)} fusion(f32[2,8,256,128]{2,3,1,0:T(8,128)S(1)} %fusion.15, f32[2,8,256,128]{2,3,1,0:T(8,128)S(1)} %fusion.17, f32[2,8,256,128]{2,3,1,0:T(8,128)S(1)} %copy-done.10, f32[2,8,256,128]{2,3,1,0:T(8,128)S(1)} %copy-done.9, bf16[512,2,128,1]{0,2,3,1:T(8,128)(2,1)S(1)} %bitcast.268, ...), kind=kOutput, calls=%fused_computation.40 | convolution fusion | flops 551026688 | bytes 18333696 | tf_op jit(solution)/shard_map/kgqs,skd->kgqd/dot_general | solution.py:49
  134.9 0.6 copy.120
  135.6 1.2 select_convert_fusion
  (64 shorter events, 6.2 us)
Async XLA Ops:
  2.9 69.5 %all-to-all-start = ((bf16[2,1,16,1,64,256]{5,4,3,1,0,2:T(8,128)(2,1)}), bf16[2,1,16,1,64,256]{5,4,3,1,0,2:T(8,128)(2,1)S(1)}, u32[]{:S(2)}, u32[]{:S(2)}) async-start(bf16[2,1,16,1,64,256]{5,4,3,1,0,2:T(8,128)(2,1)} %copy.94), calls=%async_computation | async-start | bytes 2097152 | tf_op jit(solution)/shard_map/all_to_all | solution.py:138
  28.5 21.5 %collective-permute-start = (bf16[2,256,256]{1,2,0:T(8,128)(2,1)S(1)}, bf16[2,256,256]{1,2,0:T(8,128)(2,1)}, u32[]{:S(2)}, u32[]{:S(2)}) collective-permute-start(bf16[2,256,256]{1,2,0:T(8,128)(2,1)S(1)} %copy.89), channel_id=1, source_target_pairs={{0,1},{2,3},{4,5},{6,7},{8,9},{10,11},{12,13},{14,15},{16,17},{18,... | collective-permute-start | bytes 786440 | tf_op jit(solution)/shard_map/ppermute | solution.py:20
  32.0 12.0 %copy-start.8 = (s32[8]{0:T(128)S(1)}, s32[8]{0:T(128)}, u32[]{:S(2)}) copy-start(s32[8]{0:T(128)} %param.17) | copy-start | bytes 100
  32.1 12.1 %copy-start.2 = (bf16[8,2048]{1,0:T(8,128)(2,1)S(1)}, bf16[8,2048]{1,0:T(8,128)(2,1)}, u32[]{:S(2)}) copy-start(bf16[8,2048]{1,0:T(8,128)(2,1)} %param.15) | copy-start | bytes 98308
  88.1 5.4 %copy-start.4 = (pred[512]{0:T(512)(128)(4,1)S(1)}, pred[512]{0:T(512)(128)(4,1)}, u32[]{:S(2)}) copy-start(pred[512]{0:T(512)(128)(4,1)} %get-tuple-element.3) | copy-start | bytes 1540
  88.1 10.2 %copy-start = (bf16[512,2,128]{2,1,0:T(2,128)(2,1)S(1)}, bf16[512,2,128]{2,1,0:T(2,128)(2,1)}, u32[]{:S(2)}) copy-start(bf16[512,2,128]{2,1,0:T(2,128)(2,1)} %slice.93) | copy-start | bytes 786436
  88.1 10.2 %copy-start.5 = (pred[512]{0:T(512)(128)(4,1)S(1)}, pred[512]{0:T(512)(128)(4,1)}, u32[]{:S(2)}) copy-start(pred[512]{0:T(512)(128)(4,1)} %get-tuple-element.4) | copy-start | bytes 1540
  93.6 6.3 %copy-start.6 = (pred[512]{0:T(512)(128)(4,1)S(1)}, pred[512]{0:T(512)(128)(4,1)}, u32[]{:S(2)}) copy-start(pred[512]{0:T(512)(128)(4,1)} %get-tuple-element.5) | copy-start | bytes 1540
  112.7 7.2 %copy-start.3 = (pred[512]{0:T(512)(128)(4,1)S(1)}, pred[512]{0:T(512)(128)(4,1)}, u32[]{:S(2)}) copy-start(pred[512]{0:T(512)(128)(4,1)} %get-tuple-element.2) | copy-start | bytes 1540
  114.2 13.7 %slice-start.2 = ((s8[8388608]{0:T(1024)(128)(4,1)}), s8[4194304]{0:T(1024)(128)(4,1)S(1)}, s32[]{:S(2)}) async-start(s8[8388608]{0:T(1024)(128)(4,1)} %bitcast.255), calls=%async_computation.4 | async-start | bytes 8388608
  114.2 15.9 %slice-start = ((s8[8388608]{0:T(1024)(128)(4,1)}), s8[4194304]{0:T(1024)(128)(4,1)S(1)}, s32[]{:S(2)}) async-start(s8[8388608]{0:T(1024)(128)(4,1)} %bitcast.253), calls=%async_computation.2 | async-start | bytes 8388608
  119.9 8.0 %slice-start.3 = ((s8[8388608]{0:T(1024)(128)(4,1)}), s8[4194304]{0:T(1024)(128)(4,1)S(1)}, s32[]{:S(2)}) async-start(s8[8388608]{0:T(1024)(128)(4,1)} %bitcast.255), calls=%async_computation.5 | async-start | bytes 8388608
  119.9 10.2 %slice-start.1 = ((s8[8388608]{0:T(1024)(128)(4,1)}), s8[4194304]{0:T(1024)(128)(4,1)S(1)}, s32[]{:S(2)}) async-start(s8[8388608]{0:T(1024)(128)(4,1)} %bitcast.253), calls=%async_computation.3 | async-start | bytes 8388608
  128.0 4.0 %copy-start.1 = (bf16[1,512,256]{1,2,0:T(8,128)(2,1)S(1)}, bf16[1,512,256]{1,2,0:T(8,128)(2,1)}, u32[]{:S(2)}) copy-start(bf16[1,512,256]{1,2,0:T(8,128)(2,1)} %get-tuple-element.24) | copy-start | bytes 786436
  128.0 4.0 %copy-start.9 = (f32[2,8,256,128]{2,3,1,0:T(8,128)S(1)}, f32[2,8,256,128]{2,3,1,0:T(8,128)}, u32[]{:S(2)}) copy-start(f32[2,8,256,128]{2,3,1,0:T(8,128)} %fusion.21) | copy-start | bytes 6291460
  128.0 4.0 %copy-start.10 = (f32[2,8,256,128]{2,3,1,0:T(8,128)S(1)}, f32[2,8,256,128]{2,3,1,0:T(8,128)}, u32[]{:S(2)}) copy-start(f32[2,8,256,128]{2,3,1,0:T(8,128)} %fusion.19) | copy-start | bytes 6291460
  132.0 3.5 %copy-start.7 = (pred[256]{0:T(512)(128)(4,1)S(1)}, pred[256]{0:T(512)(128)(4,1)}, u32[]{:S(2)}) copy-start(pred[256]{0:T(512)(128)(4,1)} %fusion.74) | copy-start | bytes 772
where the time goes:
time: 137 us
  matrix products  38.5 us (28%)
  starting transfers between devices  25.8 us (19%)
  local copies, waits for them, and re-layouts  24.4 us (18%)
  other arithmetic  19 us (14%)
  waiting for transfers between devices  15.7 us (11%)
  blocking collectives  10.9 us (8%)
  between operations  2.4 us (2%)
    all_to_all x1, starting transfers between devices, shards(): lax.all_to_all(hist_kv, 'grp', split_axis=2, concat_axis=1, tiled=True)  24.5 us
    dot_general x5, matrix products, block_update(): jnp.einsum('qkgd,skd->kgqs', queries, keys, preferred_element_type=jnp.fl...  18 us
    dot_general x5, matrix products, block_update(): jnp.einsum('kgqs,skd->kgqd', weights.astype(jnp.bfloat16), values, prefer...  17.7 us
    all_to_all x1, waiting for transfers between devices, shards(): lax.all_to_all(hist_kv, 'grp', split_axis=2, concat_axis=1, tiled=True)  15.7 us
    reduce_sum x3, other arithmetic, block_update(): total = total_old * factor + jnp.sum(weights, axis=-1)  14 us
    unnamed x37, local copies, waits for them, and re-layouts  12.3 us
    all_to_all x1, blocking collectives, copy_for_each(): lax.all_to_all(jnp.broadcast_to(shard[None], (devices, *shard.shape)), ax...  10.9 us
    slice x1, local copies, waits for them, and re-layouts, local_decode(): keys = dec_cache[0].reshape(requests, cached, kv_local, HD)  4.53 us
  transfers between devices with their start and end apart: 2, of which 1 were waited for; matrix products, arithmetic and copies ran while one was open for 19% of the time, Pallas kernels for 0%

commit v1 on v0

v1 whole, which is shorter than its diff:
```python
import math

import jax
import jax.numpy as jnp
from jax import lax
from jax.experimental import pallas as pl
from jax.experimental.pallas import tpu as pltpu
from jax.sharding import PartitionSpec as P

HD = 128
PAGE = 128
NEG = -1e30
MESH = pl.DeviceIdType.MESH
SCALE2 = (HD**-0.5) * math.log2(math.e)


def step_of(j):
    odd = j % 2
    return odd * ((j + 1) // 2) - (1 - odd) * (j // 2)


def nt(a, b):
    return lax.dot_general(a, b, (((1,), (0,)), ((), ())), preferred_element_type=jnp.float32)


def body(
    ng,
    q_hbm,
    nkv_hbm,
    hist_hbm,
    place,
    hlen,
    nlen,
    dq_hbm,
    dkv_hbm,
    dlen,
    out,
    dout,
    q_v,
    nkv,
    nkv_far,
    hist,
    dq_v,
    dkv,
    near,
    far,
    qt,
    kb,
    vt,
    bias,
    acc,
    top,
    total,
    local_sem,
    send_sem,
    recv_sem,
    fsend_sem,
    frecv_sem,
):
    z = lax.axis_index("grp")
    sub = lax.axis_index("sub")
    heads = qt.shape[0]
    kvh = kb.shape[0]
    group = heads // kvh
    rows = q_v.shape[0]
    half = near.shape[2]
    reqs, cached = dkv.shape[1], dkv.shape[2]

    barrier = pltpu.get_barrier_semaphore()
    for k in range(1, ng):
        pl.semaphore_signal(
            barrier, inc=1, device_id={"grp": (z + k) % ng}, device_id_type=MESH
        )
    pl.semaphore_signal(barrier, inc=1, device_id={"sub": 1 - sub}, device_id_type=MESH)

    load_hist = pltpu.make_async_copy(hist_hbm.at[:, 0, :, 0], hist, local_sem.at[0])
    load_own = pltpu.make_async_copy(hist_hbm.at[:, 0, z, 0], near.at[0], local_sem.at[1])
    load_nkv = pltpu.make_async_copy(nkv_hbm, nkv, local_sem.at[2])
    load_q = pltpu.make_async_copy(q_hbm, q_v, local_sem.at[3])
    load_dq = pltpu.make_async_copy(dq_hbm, dq_v, local_sem.at[4])
    load_dkv = pltpu.make_async_copy(dkv_hbm, dkv, local_sem.at[5])
    for load in (load_hist, load_own, load_nkv, load_q, load_dq, load_dkv):
        load.start()
    load_hist.wait()
    load_own.wait()
    load_nkv.wait()
    pl.semaphore_wait(barrier, ng)

    sends = []
    for j in range(1, ng):
        k = step_of(j)
        sends.append(
            pltpu.make_async_remote_copy(
                src_ref=hist.at[:, (z + k + ng) % ng],
                dst_ref=near.at[j],
                send_sem=send_sem.at[j],
                recv_sem=recv_sem.at[j],
                device_id={"grp": (z + k + ng) % ng},
                device_id_type=MESH,
            )
        )
        sends[-1].start()

    def forward(j):
        return pltpu.make_async_remote_copy(
            src_ref=near.at[j],
            dst_ref=far.at[j],
            send_sem=fsend_sem.at[j],
            recv_sem=frecv_sem.at[j],
            device_id={"sub": 1 - sub},
            device_id_type=MESH,
        )

    def arrival(j):
        return pltpu.make_async_remote_copy(
            src_ref=near.at[j],
            dst_ref=near.at[j],
            send_sem=send_sem.at[j],
            recv_sem=recv_sem.at[j],
            device_id={"grp": (z + 1) % ng},
            device_id_type=MESH,
        )

    swap = pltpu.make_async_remote_copy(
        src_ref=nkv,
        dst_ref=nkv_far,
        send_sem=fsend_sem.at[ng],
        recv_sem=frecv_sem.at[ng],
        device_id={"sub": 1 - sub},
        device_id_type=MESH,
    )
    swap.start()
    forward(0).start()

    load_q.wait()
    for h in range(heads):
        qt[h] = q_v[:, h * HD : (h + 1) * HD].astype(jnp.float32).T.astype(jnp.bfloat16)
    top[...] = jnp.full_like(top, NEG)
    total[...] = jnp.zeros_like(total)
    acc[...] = jnp.zeros_like(acc)

    def set_keys(keys, values):
        for g in range(kvh):
            lanes = slice(g * HD, (g + 1) * HD)
            kb[g] = jnp.concatenate([r[:, lanes] for r in keys], axis=0)
            v = jnp.concatenate([r[:, lanes] for r in values], axis=0)
            vt[g] = v.astype(jnp.float32).T.astype(jnp.bfloat16)

    def attend():
        def one(g, carry):
            k = kb[g]
            v = vt[g]
            for i in range(group):
                h = g * group + i
                s = nt(k, qt[h]) + bias[...]
                old = top[h]
                new = jnp.maximum(old, jnp.max(s, axis=0, keepdims=True))
                w = jnp.exp2((s - new) * SCALE2)
                fade = jnp.exp2((old - new) * SCALE2)
                top[h] = new
                total[h] = total[h] * fade + jnp.sum(w, axis=0, keepdims=True)
                acc[h] = acc[h] * fade + nt(v, w.astype(jnp.bfloat16))
            return carry

        lax.fori_loop(0, kvh, one, 0)

    count = nlen[0]
    square = bias.shape
    key_row = lax.broadcasted_iota(jnp.int32, square, 0)
    query_row = lax.broadcasted_iota(jnp.int32, square, 1)

    seen = (key_row <= query_row) & (sub * rows + key_row < count)
    bias[...] = jnp.where(seen, 0.0, NEG)
    set_keys([nkv.at[0]], [nkv.at[1]])
    attend()

    load_dq.wait()
    load_dkv.wait()
    dq = dq_v[...].astype(jnp.float32)
    wide = heads * reqs
    dq_rows = jnp.concatenate([dq[:, h * HD : (h + 1) * HD] for h in range(heads)], axis=0)
    dq_cols = dq_rows.T
    col = lax.broadcasted_iota(jnp.int32, (HD, wide), 1)
    col_req = col % reqs
    col_kv = col // (reqs * group)
    ds = None
    for r in range(reqs):
        blocks = [
            jnp.where((col_req == r) & (col_kv == g), dq_cols, 0.0).astype(jnp.bfloat16)
            for g in range(kvh)
        ]
        term = nt(dkv[0, r], jnp.concatenate(blocks, axis=0))
        ds = term if ds is None else ds + term
    limit_row = jnp.zeros((1, wide), jnp.int32)
    req_row = lax.broadcasted_iota(jnp.int32, (1, wide), 1) % reqs
    for r in range(reqs):
        limit_row = jnp.where(req_row == r, dlen[r], limit_row)
    dpos = lax.broadcasted_iota(jnp.int32, (cached, wide), 0)
    ds = jnp.where(dpos < limit_row, ds, NEG)
    dw = jnp.exp2((ds - jnp.max(ds, axis=0, keepdims=True)) * SCALE2)
    dwt = dw.T
    dtotal = jnp.sum(dwt, axis=1, keepdims=True)
    dwt = dwt.astype(jnp.bfloat16)
    row_req = lax.broadcasted_iota(jnp.int32, (wide, HD), 0) % reqs
    part = group * reqs
    dmix = jnp.zeros((wide, HD), jnp.float32)
    for r in range(reqs):
        full = nt(dwt, dkv[1, r])
        picked = jnp.concatenate(
            [full[g * part : (g + 1) * part, g * HD : (g + 1) * HD] for g in range(kvh)], axis=0
        )
        dmix = jnp.where(row_req == r, picked, dmix)
    dmix = dmix / dtotal
    for h in range(heads):
        dout[:, h * HD : (h + 1) * HD] = dmix[h * reqs : (h + 1) * reqs].astype(jnp.bfloat16)

    swap.wait_recv()

    @pl.when(sub == 1)
    def _():
        bias[...] = jnp.where(key_row < count, 0.0, NEG)
        set_keys([nkv_far.at[0]], [nkv_far.at[1]])
        attend()

    limit = hlen[0]
    token = lax.broadcasted_iota(jnp.int32, (half, square[1]), 0)

    def page_of(j):
        owner = (z - step_of(j) + ng) % ng
        page = 0
        for p in range(ng):
            page = page + jnp.where(place[0, p] == owner, p, 0)
        return page

    def pair(b, carry):
        for j in (2 * b, 2 * b + 1):

            @pl.when(j > 0)
            def _():
                arrival(j).wait_recv()
                forward(j).start()

        for i in range(2):
            j = 2 * b + i
            start = page_of(j) * PAGE
            for n, who in enumerate((sub, 1 - sub)):
                position = start + who * half + token
                at = (2 * i + n) * half
                bias[at : at + half] = jnp.where(position < limit, 0.0, NEG)
        for j in (2 * b, 2 * b + 1):
            forward(j).wait_recv()
        parts = [r.at[j] for j in (2 * b, 2 * b + 1) for r in (near, far)]
        set_keys([p.at[0] for p in parts], [p.at[1] for p in parts])
        attend()
        return carry

    lax.fori_loop(0, ng // 2, pair, 0)

    kept = sub * rows + lax.broadcasted_iota(jnp.int32, (1, rows), 1) < count
    for h in range(heads):
        mixed = jnp.where(kept, acc[h] / total[h], 0.0)
        out[:, h * HD : (h + 1) * HD] = mixed.T.astype(jnp.bfloat16)

    for send in sends:
        send.wait_send()
    swap.wait_send()
    for j in range(ng):
        forward(j).wait_send()


def solution(mesh):
    ng = mesh.shape["grp"]

    def shards(new_q, new_kv, hist_kv, page_place, hist_len, new_len, dec_q, dec_cache, dec_len):
        rows, width = new_q.shape
        heads = width // HD
        kvh = new_kv.shape[2] // HD
        half, lanes = hist_kv.shape[4:]
        keys = 4 * half
        anywhere = pl.BlockSpec(memory_space=pl.ANY)
        scalars = pl.BlockSpec(memory_space=pltpu.SMEM)
        vmem = pl.BlockSpec(memory_space=pltpu.VMEM)
        bf16, f32 = jnp.bfloat16, jnp.float32

        def kernel(*refs):
            body(ng, *refs)

        return pl.pallas_call(
            kernel,
            name="serve",
            out_shape=(
                jax.ShapeDtypeStruct(new_q.shape, bf16),
                jax.ShapeDtypeStruct(dec_q.shape, bf16),
            ),
            in_specs=[anywhere] * 3 + [scalars] * 3 + [anywhere] * 2 + [scalars],
            out_specs=(vmem, vmem),
            scratch_shapes=[
                pltpu.VMEM(new_q.shape, bf16),
                pltpu.VMEM(new_kv.shape, bf16),
                pltpu.VMEM(new_kv.shape, bf16),
                pltpu.VMEM((2, ng, half, lanes), bf16),
                pltpu.VMEM(dec_q.shape, bf16),
                pltpu.VMEM(dec_cache.shape, bf16),
                pltpu.VMEM((ng, 2, half, lanes), bf16),
                pltpu.VMEM((ng, 2, half, lanes), bf16),
                pltpu.VMEM((heads, HD, rows), bf16),
                pltpu.VMEM((kvh, keys, HD), bf16),
                pltpu.VMEM((kvh, HD, keys), bf16),
                pltpu.VMEM((keys, rows), f32),
                pltpu.VMEM((heads, HD, rows), f32),
                pltpu.VMEM((heads, 1, rows), f32),
                pltpu.VMEM((heads, 1, rows), f32),
                pltpu.SemaphoreType.DMA((6,)),
                pltpu.SemaphoreType.DMA((ng,)),
                pltpu.SemaphoreType.DMA((ng,)),
                pltpu.SemaphoreType.DMA((ng + 1,)),
                pltpu.SemaphoreType.DMA((ng + 1,)),
            ],
            compiler_params=pltpu.CompilerParams(
                collective_id=0, has_side_effects=True, vmem_limit_bytes=48 * 1024 * 1024
            ),
        )(new_q, new_kv, hist_kv, page_place, hist_len, new_len, dec_q, dec_cache, dec_len)

    in_specs = (
        P(("rep", "grp", "sub"), "tp"),
        P(None, ("rep", "grp", "sub"), "tp"),
        P(None, ("rep", "grp"), None, None, "sub", "tp"),
        P(("rep", "grp"), None),
        P(("rep", "grp")),
        P(("rep", "grp")),
        P(("rep", "grp", "sub"), "tp"),
        P(None, ("rep", "grp", "sub"), None, "tp"),
        P(("rep", "grp", "sub")),
    )
    out_specs = (P(("rep", "grp", "sub"), "tp"), P(("rep", "grp", "sub"), "tp"))
    return jax.shard_map(shards, mesh=mesh, in_specs=in_specs, out_specs=out_specs, check_vma=False)
```

time: 137 us -> 94.3 us (0.69)
  Pallas kernels: 0 us -> 85 us
  matrix products: 38.5 us -> 0 us
  starting transfers between devices: 25.8 us -> 0 us
  other arithmetic: 19 us -> 0 us
  local copies, waits for them, and re-layouts: 24.4 us -> 7.05 us
  waiting for transfers between devices: 15.7 us -> 0 us
  blocking collectives: 10.9 us -> 0 us
    pallas_call x0 -> x1, Pallas kernels: none -> 85 us  [shards(): pl.pallas_call(kernel, name='serve', out_shape=(jax.ShapeDtypeStruct(new_...]
    dot_general x12 -> x0, matrix products: 38.5 us -> none  [the longest x5 18 us: block_update(): jnp.einsum('qkgd,skd->kgqs', queries, keys, preferred_element_type=jnp.fl...]
    all_to_all x1 -> x0, starting transfers between devices: 24.5 us -> none  [shards(): lax.all_to_all(hist_kv, 'grp', split_axis=2, concat_axis=1, tiled=True)]
    all_to_all x1 -> x0, waiting for transfers between devices: 15.7 us -> none  [shards(): lax.all_to_all(hist_kv, 'grp', split_axis=2, concat_axis=1, tiled=True)]
    reduce_sum x5 -> x0, other arithmetic: 15 us -> none  [the longest x3 14 us: block_update(): total = total_old * factor + jnp.sum(weights, axis=-1)]
    slice x19 -> x0, local copies, waits for them, and re-layouts: 11.1 us -> none  [the longest x1 4.53 us: local_decode(): keys = dec_cache[0].reshape(requests, cached, kv_local, HD)]
    all_to_all x1 -> x0, blocking collectives: 10.9 us -> none  [copy_for_each(): lax.all_to_all(jnp.broadcast_to(shard[None], (devices, *shard.shape)), ax...]
    unnamed x37 -> x14, local copies, waits for them, and re-layouts: 12.3 us -> 7.05 us
  transfers between devices with their start and end apart: 2 -> 0, of which waited for: 1 -> 0; matrix products, arithmetic and copies ran while one was open for 19% -> 0% of each run, Pallas kernels for 0% -> 0%
where the time goes in v1:
time: 94.3 us; the launch traced here: 94 us
  Pallas kernels  85 us (90%)
  local copies, waits for them, and re-layouts  7.05 us (7%)
  between operations  1.94 us (2%)
    pallas_call x1, Pallas kernels, shards(): pl.pallas_call(kernel, name='serve', out_shape=(jax.ShapeDtypeStruct(new_...  85 us
    unnamed x14, local copies, waits for them, and re-layouts  7.05 us

profile of v1, /device:TPU:33, one launch (start us, length us, event | category | flops | bytes accessed | tf_op | source)
XLA Modules:
  0.0 94.0 jit_solution(2790853815323481204)
XLA Ops:
  1.9 0.0 copy-start
  1.9 1.2 %copy-done = bf16[256,2048]{1,0:T(8,128)(2,1)S(1)} copy-done((bf16[256,2048]{1,0:T(8,128)(2,1)S(1)}, bf16[256,2048]{1,0:T(8,128)(2,1)}, u32[]{:S(2)}) %copy-start) | copy-done | bytes 1048600
  3.1 0.0 copy-start.1
  3.2 1.2 %copy-done.1 = bf16[2,1,16,1,64,256]{5,4,3,2,1,0:T(8,128)(2,1)S(1)} copy-done((bf16[2,1,16,1,64,256]{5,4,3,2,1,0:T(8,128)(2,1)S(1)}, bf16[2,1,16,1,64,256]{5,4,3,2,1,0:T(8,128)(2,1)}, u32[]{:S(2)}) %copy-start.1) | copy-done | bytes 1048600
  4.4 0.0 copy-start.2
  4.4 0.9 %copy-done.2 = bf16[2,256,256]{2,1,0:T(8,128)(2,1)S(1)} copy-done((bf16[2,256,256]{2,1,0:T(8,128)(2,1)S(1)}, bf16[2,256,256]{2,1,0:T(8,128)(2,1)}, u32[]{:S(2)}) %copy-start.2) | copy-done | bytes 262168
  5.3 0.0 copy-start.3
  5.3 0.8 copy-done.3
  6.1 0.0 copy-start.4
  6.1 0.7 copy-done.4
  6.7 0.0 copy-start.5
  6.7 0.7 copy-done.5
  7.4 85.0 %serve.1 = (bf16[256,2048]{1,0:T(8,128)(2,1)S(1)}, bf16[8,2048]{1,0:T(8,128)(2,1)S(1)}) custom-call(bf16[256,2048]{1,0:T(8,128)(2,1)S(1)} %copy-done, bf16[2,256,256]{2,1,0:T(8,128)(2,1)S(1)} %copy-done.2, bf16[2,1,16,1,64,256]{5,4,3,2,1,0:T(8,128)(2,1)S(1)} %copy-done.1, s32[1,16]{1,0:T(1,128)S(1)} %copy-done.4, s32[1]{0:T(128)S(6)} %copy.13.refs_4_, ...), custom_call_target="tpu_custom_call" | custom-call | tf_op jit(solution)/shard_map/serve/pallas_call | solution.py:288
  92.4 1.0 %copy.15 = bf16[256,2048]{1,0:T(8,128)(2,1)} copy(bf16[256,2048]{1,0:T(8,128)(2,1)S(1)} %get-tuple-element.4) | data formatting | bytes 2097152
  93.4 0.6 copy.16
Async XLA Ops:
  1.9 1.2 %copy-start = (bf16[256,2048]{1,0:T(8,128)(2,1)S(1)}, bf16[256,2048]{1,0:T(8,128)(2,1)}, u32[]{:S(2)}) copy-start(bf16[256,2048]{1,0:T(8,128)(2,1)} %refs_0_.1) | copy-start | bytes 3145732
  3.1 1.2 %copy-start.1 = (bf16[2,1,16,1,64,256]{5,4,3,2,1,0:T(8,128)(2,1)S(1)}, bf16[2,1,16,1,64,256]{5,4,3,2,1,0:T(8,128)(2,1)}, u32[]{:S(2)}) copy-start(bf16[2,1,16,1,64,256]{5,4,3,2,1,0:T(8,128)(2,1)} %refs_2_.1) | copy-start | bytes 3145732
  4.4 0.9 %copy-start.2 = (bf16[2,256,256]{2,1,0:T(8,128)(2,1)S(1)}, bf16[2,256,256]{2,1,0:T(8,128)(2,1)}, u32[]{:S(2)}) copy-start(bf16[2,256,256]{2,1,0:T(8,128)(2,1)} %refs_1_.1) | copy-start | bytes 786436
  5.3 0.8 copy-start.3
  6.1 0.7 copy-start.4
  6.7 0.7 copy-start.5

commit v2 on v1

--- a/solution.py
+++ b/solution.py
@@ -28,12 +28,12 @@
     q_hbm,
     nkv_hbm,
     hist_hbm,
-    place,
+    place_hbm,
     hlen,
     nlen,
     dq_hbm,
     dkv_hbm,
-    dlen,
+    dlen_hbm,
     out,
     dout,
     q_v,
@@ -47,10 +47,11 @@
     qt,
     kb,
     vt,
-    bias,
     acc,
     top,
     total,
+    place,
+    dlen,
     local_sem,
     send_sem,
     recv_sem,
@@ -79,7 +80,11 @@
     load_q = pltpu.make_async_copy(q_hbm, q_v, local_sem.at[3])
     load_dq = pltpu.make_async_copy(dq_hbm, dq_v, local_sem.at[4])
     load_dkv = pltpu.make_async_copy(dkv_hbm, dkv, local_sem.at[5])
-    for load in (load_hist, load_own, load_nkv, load_q, load_dq, load_dkv):
+    load_scalars = [
+        pltpu.make_async_copy(place_hbm, place, local_sem.at[6]),
+        pltpu.make_async_copy(dlen_hbm, dlen, local_sem.at[7]),
+    ]
+    for load in (load_hist, load_own, load_nkv, load_q, load_dq, *load_scalars, load_dkv):
         load.start()
     load_hist.wait()
     load_own.wait()
@@ -133,46 +138,71 @@
     forward(0).start()
 
     load_q.wait()
+    for load in load_scalars:
+        load.wait()
+    one_row = (lax.broadcasted_iota(jnp.int32, (HD, rows), 0) == 0).astype(jnp.float32)
+    one_row = one_row.astype(jnp.bfloat16)
     for h in range(heads):
-        qt[h] = q_v[:, h * HD : (h + 1) * HD].astype(jnp.float32).T.astype(jnp.bfloat16)
+        scaled = q_v[:, h * HD : (h + 1) * HD].astype(jnp.float32) * SCALE2
+        qt[h, :HD] = scaled.T.astype(jnp.bfloat16)
+        qt[h, HD:] = one_row
     top[...] = jnp.full_like(top, NEG)
     total[...] = jnp.zeros_like(total)
     acc[...] = jnp.zeros_like(acc)
 
-    def set_keys(keys, values):
+    def set_keys(keys, values, biases):
         for g in range(kvh):
             lanes = slice(g * HD, (g + 1) * HD)
-            kb[g] = jnp.concatenate([r[:, lanes] for r in keys], axis=0)
+            kb[g, :, :HD] = jnp.concatenate([r[:, lanes] for r in keys], axis=0)
+            kb[g, :, HD:] = jnp.concatenate(biases, axis=0)
             v = jnp.concatenate([r[:, lanes] for r in values], axis=0)
             vt[g] = v.astype(jnp.float32).T.astype(jnp.bfloat16)
 
-    def attend():
-        def one(g, carry):
-            k = kb[g]
-            v = vt[g]
-            for i in range(group):
-                h = g * group + i
-                s = nt(k, qt[h]) + bias[...]
-                old = top[h]
-                new = jnp.maximum(old, jnp.max(s, axis=0, keepdims=True))
-                w = jnp.exp2((s - new) * SCALE2)
-                fade = jnp.exp2((old - new) * SCALE2)
-                top[h] = new
-                total[h] = total[h] * fade + jnp.sum(w, axis=0, keepdims=True)
-                acc[h] = acc[h] * fade + nt(v, w.astype(jnp.bfloat16))
-            return carry
-
-        lax.fori_loop(0, kvh, one, 0)
+    span = kb.shape[1]
+
+    def attend(causal):
+        def score(h):
+            s = nt(kb[h // group], qt[h])
+            if causal:
+                key = lax.broadcasted_iota(jnp.int32, s.shape, 0)
+                query = lax.broadcasted_iota(jnp.int32, s.shape, 1)
+                s = jnp.where(key <= query, s, NEG)
+            return s.reshape(span // 8, 8, rows)
+
+        def weigh(h, s):
+            old = top[h]
+            new = jnp.maximum(old, jnp.max(s, axis=0))
+            for shift in (4, 2, 1):
+                new = jnp.maximum(new, pltpu.roll(new, shift, 0))
+            fade = jnp.exp2(old - new)
+            w = jnp.exp2(s - new[None])
+            top[h] = new
+            total[h] = total[h] * fade + jnp.sum(w, axis=0)
+            return w.reshape(span, rows).astype(jnp.bfloat16), fade
+
+        def mix(h, w, fade):
+            kept = acc[h].reshape(HD // 8, 8, rows) * fade[None]
+            acc[h] = kept.reshape(HD, rows) + nt(vt[h // group], w)
+
+        s = score(0)
+        last = None
+        for h in range(heads):
+            ahead = score(h + 1) if h + 1 < heads else None
+            w, fade = weigh(h, s)
+            if last is not None:
+                mix(*last)
+            last = (h, w, fade)
+            s = ahead
+        mix(*last)
 
     count = nlen[0]
-    square = bias.shape
-    key_row = lax.broadcasted_iota(jnp.int32, square, 0)
-    query_row = lax.broadcasted_iota(jnp.int32, square, 1)
-
-    seen = (key_row <= query_row) & (sub * rows + key_row < count)
-    bias[...] = jnp.where(seen, 0.0, NEG)
-    set_keys([nkv.at[0]], [nkv.at[1]])
-    attend()
+
+    def hide(shape, start, limit):
+        position = start + lax.broadcasted_iota(jnp.int32, shape, 0)
+        return jnp.where(position < limit, 0.0, NEG).astype(jnp.bfloat16)
+
+    set_keys([nkv.at[0]], [nkv.at[1]], [hide((rows, HD), sub * rows, count)])
+    attend(True)
 
     load_dq.wait()
     load_dkv.wait()
@@ -218,12 +248,10 @@
 
     @pl.when(sub == 1)
     def _():
-        bias[...] = jnp.where(key_row < count, 0.0, NEG)
-        set_keys([nkv_far.at[0]], [nkv_far.at[1]])
-        attend()
+        set_keys([nkv_far.at[0]], [nkv_far.at[1]], [hide((rows, HD), 0, count)])
+        attend(False)
 
     limit = hlen[0]
-    token = lax.broadcasted_iota(jnp.int32, (half, square[1]), 0)
 
     def page_of(j):
         owner = (z - step_of(j) + ng) % ng
@@ -232,33 +260,47 @@
             page = page + jnp.where(place[0, p] == owner, p, 0)
         return page
 
+    def take(b):
+        for j in (2 * b, 2 * b + 1):
+            arrival(j).wait_recv()
+            forward(j).start()
+
+    def use(b):
+        slots = (2 * b, 2 * b + 1)
+        biases = [
+            hide((half, HD), page_of(j) * PAGE + who * half, limit)
+            for j in slots
+            for who in (sub, 1 - sub)
+        ]
+        for j in slots:
+            forward(j).wait_recv()
+        parts = [r.at[j] for j in slots for r in (near, far)]
+        set_keys([p.at[0] for p in parts], [p.at[1] for p in parts], biases)
+        attend(False)
+
+    arrival(1).wait_recv()
+    forward(1).start()
+    pairs = ng // 2
+
     def pair(b, carry):
-        for j in (2 * b, 2 * b + 1):
-
-            @pl.when(j > 0)
-            def _():
-                arrival(j).wait_recv()
-                forward(j).start()
-
-        for i in range(2):
-            j = 2 * b + i
-            start = page_of(j) * PAGE
-            for n, who in enumerate((sub, 1 - sub)):
-                position = start + who * half + token
-                at = (2 * i + n) * half
-                bias[at : at + half] = jnp.where(position < limit, 0.0, NEG)
-        for j in (2 * b, 2 * b + 1):
-            forward(j).wait_recv()
-        parts = [r.at[j] for j in (2 * b, 2 * b + 1) for r in (near, far)]
-        set_keys([p.at[0] for p in parts], [p.at[1] for p in parts])
-        attend()
+        @pl.when(b < pairs - 1)
+        def _():
+            take(b)
+
+        use(b - 1)
+
+        @pl.when(b == pairs - 1)
+        def _():
+            take(b)
+
         return carry
 
-    lax.fori_loop(0, ng // 2, pair, 0)
+    lax.fori_loop(1, pairs, pair, 0)
+    use(pairs - 1)
 
     kept = sub * rows + lax.broadcasted_iota(jnp.int32, (1, rows), 1) < count
     for h in range(heads):
-        mixed = jnp.where(kept, acc[h] / total[h], 0.0)
+        mixed = jnp.where(kept, acc[h] / jnp.sum(total[h], axis=0, keepdims=True), 0.0)
         out[:, h * HD : (h + 1) * HD] = mixed.T.astype(jnp.bfloat16)
 
     for send in sends:
@@ -277,10 +319,13 @@
         kvh = new_kv.shape[2] // HD
         half, lanes = hist_kv.shape[4:]
         keys = 4 * half
-        anywhere = pl.BlockSpec(memory_space=pl.ANY)
+        anywhere = pl.BlockSpec(memory_space=pltpu.HBM)
         scalars = pl.BlockSpec(memory_space=pltpu.SMEM)
         vmem = pl.BlockSpec(memory_space=pltpu.VMEM)
         bf16, f32 = jnp.bfloat16, jnp.float32
+
+        def keep(x):
+            return pltpu.with_memory_space_constraint(x, pltpu.HBM)
 
         def kernel(*refs):
             body(ng, *refs)
@@ -292,7 +337,7 @@
                 jax.ShapeDtypeStruct(new_q.shape, bf16),
                 jax.ShapeDtypeStruct(dec_q.shape, bf16),
             ),
-            in_specs=[anywhere] * 3 + [scalars] * 3 + [anywhere] * 2 + [scalars],
+            in_specs=[anywhere] * 4 + [scalars] * 2 + [anywhere] * 3,
             out_specs=(vmem, vmem),
             scratch_shapes=[
                 pltpu.VMEM(new_q.shape, bf16),
@@ -303,23 +348,29 @@
                 pltpu.VMEM(dec_cache.shape, bf16),
                 pltpu.VMEM((ng, 2, half, lanes), bf16),
                 pltpu.VMEM((ng, 2, half, lanes), bf16),
-                pltpu.VMEM((heads, HD, rows), bf16),
-                pltpu.VMEM((kvh, keys, HD), bf16),
+                pltpu.VMEM((heads, 2 * HD, rows), bf16),
+                pltpu.VMEM((kvh, keys, 2 * HD), bf16),
                 pltpu.VMEM((kvh, HD, keys), bf16),
-                pltpu.VMEM((keys, rows), f32),
                 pltpu.VMEM((heads, HD, rows), f32),
-                pltpu.VMEM((heads, 1, rows), f32),
-                pltpu.VMEM((heads, 1, rows), f32),
-                pltpu.SemaphoreType.DMA((6,)),
+                pltpu.VMEM((heads, 8, rows), f32),
+                pltpu.VMEM((heads, 8, rows), f32),
+                pltpu.SMEM(page_place.shape, jnp.int32),
+                pltpu.SMEM(dec_len.shape, jnp.int32),
+                pltpu.SemaphoreType.DMA((8,)),
                 pltpu.SemaphoreType.DMA((ng,)),
                 pltpu.SemaphoreType.DMA((ng,)),
                 pltpu.SemaphoreType.DMA((ng + 1,)),
                 pltpu.SemaphoreType.DMA((ng + 1,)),
             ],
             compiler_params=pltpu.CompilerParams(
-                collective_id=0, has_side_effects=True, vmem_limit_bytes=48 * 1024 * 1024
+                collective_id=0, has_side_effects=True, vmem_limit_bytes=40 * 1024 * 1024
             ),
-        )(new_q, new_kv, hist_kv, page_place, hist_len, new_len, dec_q, dec_cache, dec_len)
+        )(
+            *(keep(x) for x in (new_q, new_kv, hist_kv, page_place)),
+            hist_len,
+            new_len,
+            *(keep(x) for x in (dec_q, dec_cache, dec_len)),
+        )
 
     in_specs = (
         P(("rep", "grp", "sub"), "tp"),

time: 94.3 us -> 82 us (0.87)
  Pallas kernels: 85 us -> 77.7 us
  local copies, waits for them, and re-layouts: 7.05 us -> 1.59 us
    pallas_call x1, Pallas kernels: 85 us -> 77.7 us  [shards(): pl.pallas_call(kernel, name='serve', out_shape=(jax.ShapeDtypeStruct(new_...]
    unnamed x14 -> x2, local copies, waits for them, and re-layouts: 7.05 us -> 1.59 us
where the time goes in v2:
time: 82 us; the launch traced here: 81.2 us
  Pallas kernels  77.7 us (95%)
  between operations  1.93 us (2%)
  local copies, waits for them, and re-layouts  1.59 us (2%)
    pallas_call x1, Pallas kernels, shards(): pl.pallas_call(kernel, name='serve', out_shape=(jax.ShapeDtypeStruct(new_...  77.7 us

profile of v2, /device:TPU:33, one launch (start us, length us, event | category | flops | bytes accessed | tf_op | source)
XLA Modules:
  0.0 81.2 jit_solution(12966699566341000211)
XLA Ops:
  1.9 77.7 %serve.1 = (bf16[256,2048]{1,0:T(8,128)(2,1)S(1)}, bf16[8,2048]{1,0:T(8,128)(2,1)S(1)}) custom-call(bf16[256,2048]{1,0:T(8,128)(2,1)} %refs_0_.1, bf16[2,256,256]{2,1,0:T(8,128)(2,1)} %refs_1_.1, bf16[2,1,16,1,64,256]{5,4,3,2,1,0:T(8,128)(2,1)} %refs_2_.1, s32[1,16]{1,0:T(1,128)} %refs_3_.1, s32[1]{0:T(128)S(6)} %copy.13.refs_4_, s32[1]{0:T(128)S(6)} %copy.14.refs_5_, ...), custom_call_target="tpu_custom_call" | custom-call | tf_op jit(solution)/shard_map/serve/pallas_call | solution.py:333
  79.6 1.0 %copy.15 = bf16[256,2048]{1,0:T(8,128)(2,1)} copy(bf16[256,2048]{1,0:T(8,128)(2,1)S(1)} %get-tuple-element.4) | data formatting | bytes 2097152
  80.6 0.6 copy.16

commit v3 on v2

--- a/solution.py
+++ b/solution.py
@@ -14,9 +14,10 @@
 SCALE2 = (HD**-0.5) * math.log2(math.e)
 
 
-def step_of(j):
+def source_of(j, z, ng):
     odd = j % 2
-    return odd * ((j + 1) // 2) - (1 - odd) * (j // 2)
+    step = odd * ((j + 1) // 2) - (1 - odd) * (j // 2)
+    return (z + step + ng) % ng
 
 
 def nt(a, b):
@@ -57,6 +58,7 @@
     recv_sem,
     fsend_sem,
     frecv_sem,
+    in_sem,
 ):
     z = lax.axis_index("grp")
     sub = lax.axis_index("sub")
@@ -67,15 +69,27 @@
     half = near.shape[2]
     reqs, cached = dkv.shape[1], dkv.shape[2]
 
+    low = ng // 2
+    early = low - 3
+    first = jnp.where(lax.axis_index("tp") == 0, ng - 2, low)
     barrier = pltpu.get_barrier_semaphore()
-    for k in range(1, ng):
-        pl.semaphore_signal(
-            barrier, inc=1, device_id={"grp": (z + k) % ng}, device_id_type=MESH
-        )
+
+    def greet(d):
+        pl.semaphore_signal(barrier, inc=1, device_id={"grp": d}, device_id_type=MESH)
+
+    def tell(sem, d):
+        pl.semaphore_signal(sem, inc=1, device_id={"grp": d}, device_id_type=MESH)
+
     pl.semaphore_signal(barrier, inc=1, device_id={"sub": 1 - sub}, device_id_type=MESH)
 
+    for d in range(low, ng):
+
+        @pl.when((z == 0) & ((first == low) | (first == d)))
+        def _():
+            greet(d)
+
     load_hist = pltpu.make_async_copy(hist_hbm.at[:, 0, :, 0], hist, local_sem.at[0])
-    load_own = pltpu.make_async_copy(hist_hbm.at[:, 0, z, 0], near.at[0], local_sem.at[1])
+    load_own = pltpu.make_async_copy(hist_hbm.at[:, 0, z, 0], near.at[z], local_sem.at[1])
     load_nkv = pltpu.make_async_copy(nkv_hbm, nkv, local_sem.at[2])
     load_q = pltpu.make_async_copy(q_hbm, q_v, local_sem.at[3])
     load_dq = pltpu.make_async_copy(dq_hbm, dq_v, local_sem.at[4])
@@ -89,40 +103,85 @@
     load_hist.wait()
     load_own.wait()
     load_nkv.wait()
-    pl.semaphore_wait(barrier, ng)
-
-    sends = []
-    for j in range(1, ng):
-        k = step_of(j)
-        sends.append(
-            pltpu.make_async_remote_copy(
-                src_ref=hist.at[:, (z + k + ng) % ng],
-                dst_ref=near.at[j],
-                send_sem=send_sem.at[j],
-                recv_sem=recv_sem.at[j],
-                device_id={"grp": (z + k + ng) % ng},
-                device_id_type=MESH,
-            )
+    pred = jnp.where(z >= 2, 1, 0)
+    zero = jnp.where(((first == low) & (z >= low)) | (first == z), 1, 0)
+    pl.semaphore_wait(barrier, 1 + pred + zero)
+
+    def send(d):
+        return pltpu.make_async_remote_copy(
+            src_ref=hist.at[:, d],
+            dst_ref=near.at[z],
+            send_sem=send_sem.at[d],
+            recv_sem=recv_sem.at[z],
+            device_id={"grp": d},
+            device_id_type=MESH,
         )
-        sends[-1].start()
-
-    def forward(j):
+
+    @pl.when((z >= 1) & (z < ng - 1))
+    def _():
+        greet(z + 1)
+
+    for d in range(ng - 1):
+
+        @pl.when(z >= first if d == 0 else z > d)
+        def _():
+            tell(in_sem.at[z], d)
+
+    def give(when, d):
+        @pl.when(when)
+        def _():
+            send(d).start()
+
+    for t in range(low):
+        straight = (z >= first) | ((first == low) & (z >= low))
+        give(straight & (t <= z - low), t)
+        if t < low - 1:
+            down = z - 1 - t
+            give((z >= low) | ((z >= 1) & (down >= 1)), down)
+
+    def hear(d):
+        pl.semaphore_wait(in_sem.at[d], 1)
+
+    def reach_up():
+        for d in range(2, low):
+
+            @pl.when((z >= 1) & (z < d))
+            def _():
+                hear(d)
+                send(d).start()
+
+        hear(first)
+        give(z >= 1, 0)
+        for t in range(1, low):
+            give((z == 0) & (t < first), t)
+            if low < ng - 1 - t:
+                give((z == 0) & (ng - 1 - t < first), ng - 1 - t)
+        give((z == 0) & (low < first), low)
+        for d in range(low, ng):
+
+            @pl.when(((z >= 1) | (d >= first)) & (d != first))
+            def _():
+                hear(d)
+
+            give((z >= 1) | (d >= first), d)
+
+    def forward(s):
         return pltpu.make_async_remote_copy(
-            src_ref=near.at[j],
-            dst_ref=far.at[j],
-            send_sem=fsend_sem.at[j],
-            recv_sem=frecv_sem.at[j],
+            src_ref=near.at[s],
+            dst_ref=far.at[s],
+            send_sem=fsend_sem.at[s],
+            recv_sem=frecv_sem.at[s],
             device_id={"sub": 1 - sub},
             device_id_type=MESH,
         )
 
-    def arrival(j):
+    def arrival(s):
         return pltpu.make_async_remote_copy(
-            src_ref=near.at[j],
-            dst_ref=near.at[j],
-            send_sem=send_sem.at[j],
-            recv_sem=recv_sem.at[j],
-            device_id={"grp": (z + 1) % ng},
+            src_ref=near.at[s],
+            dst_ref=near.at[s],
+            send_sem=send_sem.at[s],
+            recv_sem=recv_sem.at[s],
+            device_id={"sub": 1 - sub},
             device_id_type=MESH,
         )
 
@@ -135,7 +194,28 @@
         device_id_type=MESH,
     )
     swap.start()
-    forward(0).start()
+    forward(z).start()
+
+    @pl.when(z >= low)
+    def _():
+        @pl.when((first != low) & (z < first))
+        def _():
+            hear(first)
+
+        for t in range(low):
+            give((first != low) & (z < first) & (t <= z - low), t)
+        for d in range(low + 1, ng):
+
+            @pl.when((z < d) & (d != first))
+            def _():
+                hear(d)
+
+            give(z < d, d)
+
+    @pl.when((z >= early) & (z < low))
+    def _():
+        reach_up()
+
 
     load_q.wait()
     for load in load_scalars:
@@ -160,7 +240,7 @@
 
     span = kb.shape[1]
 
-    def attend(causal):
+    def attend(causal, last_block=False):
         def score(h):
             s = nt(kb[h // group], qt[h])
             if causal:
@@ -182,7 +262,13 @@
 
         def mix(h, w, fade):
             kept = acc[h].reshape(HD // 8, 8, rows) * fade[None]
-            acc[h] = kept.reshape(HD, rows) + nt(vt[h // group], w)
+            mixed = kept.reshape(HD, rows) + nt(vt[h // group], w)
+            if last_block:
+                mixed = mixed / jnp.sum(total[h], axis=0, keepdims=True)
+                mixed = jnp.where(live, mixed, 0.0)
+                out[:, h * HD : (h + 1) * HD] = mixed.T.astype(jnp.bfloat16)
+            else:
+                acc[h] = mixed
 
         s = score(0)
         last = None
@@ -196,6 +282,7 @@
         mix(*last)
 
     count = nlen[0]
+    live = sub * rows + lax.broadcasted_iota(jnp.int32, (1, rows), 1) < count
 
     def hide(shape, start, limit):
         position = start + lax.broadcasted_iota(jnp.int32, shape, 0)
@@ -244,6 +331,10 @@
     for h in range(heads):
         dout[:, h * HD : (h + 1) * HD] = dmix[h * reqs : (h + 1) * reqs].astype(jnp.bfloat16)
 
+    @pl.when(z < early)
+    def _():
+        reach_up()
+
     swap.wait_recv()
 
     @pl.when(sub == 1)
@@ -253,33 +344,34 @@
 
     limit = hlen[0]
 
-    def page_of(j):
-        owner = (z - step_of(j) + ng) % ng
+    def page_of(owner):
         page = 0
         for p in range(ng):
             page = page + jnp.where(place[0, p] == owner, p, 0)
         return page
 
     def take(b):
-        for j in (2 * b, 2 * b + 1):
-            arrival(j).wait_recv()
-            forward(j).start()
-
-    def use(b):
-        slots = (2 * b, 2 * b + 1)
+        for s in (source_of(2 * b, z, ng), source_of(2 * b + 1, z, ng)):
+            arrival(s).wait_recv()
+            forward(s).start()
+
+    def use(b, last_block=False):
+        order = (2 * b, 2 * b + 1)
+        slots = [source_of(j, z, ng) for j in order]
         biases = [
             hide((half, HD), page_of(j) * PAGE + who * half, limit)
             for j in slots
             for who in (sub, 1 - sub)
         ]
-        for j in slots:
-            forward(j).wait_recv()
-        parts = [r.at[j] for j in slots for r in (near, far)]
+        for s in slots:
+            forward(s).wait_recv()
+        parts = [r.at[s] for s in slots for r in (near, far)]
         set_keys([p.at[0] for p in parts], [p.at[1] for p in parts], biases)
-        attend(False)
-
-    arrival(1).wait_recv()
-    forward(1).start()
+        attend(False, last_block)
+
+    second = source_of(1, z, ng)
+    arrival(second).wait_recv()
+    forward(second).start()
     pairs = ng // 2
 
     def pair(b, carry):
@@ -296,18 +388,16 @@
         return carry
 
     lax.fori_loop(1, pairs, pair, 0)
-    use(pairs - 1)
-
-    kept = sub * rows + lax.broadcasted_iota(jnp.int32, (1, rows), 1) < count
-    for h in range(heads):
-        mixed = jnp.where(kept, acc[h] / jnp.sum(total[h], axis=0, keepdims=True), 0.0)
-        out[:, h * HD : (h + 1) * HD] = mixed.T.astype(jnp.bfloat16)
-
-    for send in sends:
-        send.wait_send()
+    use(pairs - 1, True)
+
+    for d in range(ng):
+
+        @pl.when(z != d)
+        def _():
+            send(d).wait_send()
+
+        forward(d).wait_send()
     swap.wait_send()
-    for j in range(ng):
-        forward(j).wait_send()
 
 
 def solution(mesh):
@@ -361,6 +451,7 @@
                 pltpu.SemaphoreType.DMA((ng,)),
                 pltpu.SemaphoreType.DMA((ng + 1,)),
                 pltpu.SemaphoreType.DMA((ng + 1,)),
+                pltpu.SemaphoreType.REGULAR((ng,)),
             ],
             compiler_params=pltpu.CompilerParams(
                 collective_id=0, has_side_effects=True, vmem_limit_bytes=40 * 1024 * 1024

time: 82 us -> 77.9 us (0.950)
  the two profiles are of different devices: /device:TPU:33 before, /device:TPU:297 now
where the time goes in v3:
time: 77.9 us; the launch traced here: 77.8 us
  Pallas kernels  74.3 us (95%)
  between operations  1.93 us (2%)
  local copies, waits for them, and re-layouts  1.59 us (2%)
    pallas_call x1, Pallas kernels, shards(): pl.pallas_call(kernel, name='serve', out_shape=(jax.ShapeDtypeStruct(new_...  74.3 us
    unnamed x2, local copies, waits for them, and re-layouts  1.59 us

profile of v3, /device:TPU:297, one launch (start us, length us, event | category | flops | bytes accessed | tf_op | source)
XLA Modules:
  0.0 77.8 jit_solution(1556975998973704705)
XLA Ops:
  1.9 74.3 %serve.1 = (bf16[256,2048]{1,0:T(8,128)(2,1)S(1)}, bf16[8,2048]{1,0:T(8,128)(2,1)S(1)}) custom-call(bf16[256,2048]{1,0:T(8,128)(2,1)} %refs_0_.1, bf16[2,256,256]{2,1,0:T(8,128)(2,1)} %refs_1_.1, bf16[2,1,16,1,64,256]{5,4,3,2,1,0:T(8,128)(2,1)} %refs_2_.1, s32[1,16]{1,0:T(1,128)} %refs_3_.1, s32[1]{0:T(128)S(6)} %copy.13.refs_4_, s32[1]{0:T(128)S(6)} %copy.14.refs_5_, ...), custom_call_target="tpu_custom_call" | custom-call | tf_op jit(solution)/shard_map/serve/pallas_call | solution.py:423
  76.2 1.0 %copy.15 = bf16[256,2048]{1,0:T(8,128)(2,1)} copy(bf16[256,2048]{1,0:T(8,128)(2,1)S(1)} %get-tuple-element.4) | data formatting | bytes 2097152
  77.2 0.6 copy.16

commit v4 on v3

--- a/solution.py
+++ b/solution.py
@@ -71,6 +71,7 @@
 
     low = ng // 2
     early = low - 3
+    nigh = low + 3
     first = jnp.where(lax.axis_index("tp") == 0, ng - 2, low)
     barrier = pltpu.get_barrier_semaphore()
 
@@ -134,6 +135,8 @@
 
     for t in range(low):
         straight = (z >= first) | ((first == low) & (z >= low))
+        if t > 0:
+            straight |= z >= nigh
         give(straight & (t <= z - low), t)
         if t < low - 1:
             down = z - 1 - t
@@ -203,7 +206,8 @@
             hear(first)
 
         for t in range(low):
-            give((first != low) & (z < first) & (t <= z - low), t)
+            held = (first != low) & (z < first) & (t <= z - low)
+            give(held if t == 0 else held & (z < nigh), t)
         for d in range(low + 1, ng):
 
             @pl.when((z < d) & (d != first))

time: 77.9 us -> 83.9 us (1.077)
  the two profiles are of different devices: /device:TPU:297 before, /device:TPU:33 now
where the time goes in v4:
time: 83.9 us; the launch traced here: 83.7 us
  Pallas kernels  80.2 us (96%)
  between operations  1.93 us (2%)
  local copies, waits for them, and re-layouts  1.59 us (2%)
    pallas_call x1, Pallas kernels, shards(): pl.pallas_call(kernel, name='serve', out_shape=(jax.ShapeDtypeStruct(new_...  80.2 us

profile of v4, /device:TPU:33, one launch (start us, length us, event | category | flops | bytes accessed | tf_op | source)
XLA Modules:
  0.0 83.7 jit_solution(9356883877131098907)
XLA Ops:
  1.9 80.2 %serve.1 = (bf16[256,2048]{1,0:T(8,128)(2,1)S(1)}, bf16[8,2048]{1,0:T(8,128)(2,1)S(1)}) custom-call(bf16[256,2048]{1,0:T(8,128)(2,1)} %refs_0_.1, bf16[2,256,256]{2,1,0:T(8,128)(2,1)} %refs_1_.1, bf16[2,1,16,1,64,256]{5,4,3,2,1,0:T(8,128)(2,1)} %refs_2_.1, s32[1,16]{1,0:T(1,128)} %refs_3_.1, s32[1]{0:T(128)S(6)} %copy.13.refs_4_, s32[1]{0:T(128)S(6)} %copy.14.refs_5_, ...), custom_call_target="tpu_custom_call" | custom-call | tf_op jit(solution)/shard_map/serve/pallas_call | solution.py:427
  82.1 1.0 %copy.15 = bf16[256,2048]{1,0:T(8,128)(2,1)} copy(bf16[256,2048]{1,0:T(8,128)(2,1)S(1)} %get-tuple-element.4) | data formatting | bytes 2097152
  83.1 0.6 copy.16

commit v5 on v3

--- a/solution.py
+++ b/solution.py
@@ -150,8 +150,14 @@
                 hear(d)
                 send(d).start()
 
-        hear(first)
-        give(z >= 1, 0)
+        soon = (first == low) | (z == 0) | (z >= early)
+        later = jnp.logical_not(soon)
+
+        @pl.when(soon)
+        def _():
+            hear(first)
+
+        give(soon & (z >= 1), 0)
         for t in range(1, low):
             give((z == 0) & (t < first), t)
             if low < ng - 1 - t:
@@ -159,11 +165,13 @@
         give((z == 0) & (low < first), low)
         for d in range(low, ng):
 
-            @pl.when(((z >= 1) | (d >= first)) & (d != first))
+            @pl.when(((z >= 1) | (d >= first)) & ((d != first) | later))
             def _():
                 hear(d)
 
             give((z >= 1) | (d >= first), d)
+            if d == ng - 2:
+                give(later, 0)
 
     def forward(s):
         return pltpu.make_async_remote_copy(

time: 77.9 us -> 93.5 us (1.20)
  the two profiles are of different devices: /device:TPU:297 before, /device:TPU:33 now
where the time goes in v5:
time: 93.5 us; the launch traced here: 93.4 us
  Pallas kernels  89.8 us (96%)
  between operations  1.93 us (2%)
  local copies, waits for them, and re-layouts  1.59 us (2%)
    pallas_call x1, Pallas kernels, shards(): pl.pallas_call(kernel, name='serve', out_shape=(jax.ShapeDtypeStruct(new_...  89.8 us

profile of v5, /device:TPU:33, one launch (start us, length us, event | category | flops | bytes accessed | tf_op | source)
XLA Modules:
  0.0 93.4 jit_solution(18184372768329215188)
XLA Ops:
  1.9 89.8 %serve.1 = (bf16[256,2048]{1,0:T(8,128)(2,1)S(1)}, bf16[8,2048]{1,0:T(8,128)(2,1)S(1)}) custom-call(bf16[256,2048]{1,0:T(8,128)(2,1)} %refs_0_.1, bf16[2,256,256]{2,1,0:T(8,128)(2,1)} %refs_1_.1, bf16[2,1,16,1,64,256]{5,4,3,2,1,0:T(8,128)(2,1)} %refs_2_.1, s32[1,16]{1,0:T(1,128)} %refs_3_.1, s32[1]{0:T(128)S(6)} %copy.13.refs_4_, s32[1]{0:T(128)S(6)} %copy.14.refs_5_, ...), custom_call_target="tpu_custom_call" | custom-call | tf_op jit(solution)/shard_map/serve/pallas_call | solution.py:431
  91.8 1.0 %copy.15 = bf16[256,2048]{1,0:T(8,128)(2,1)} copy(bf16[256,2048]{1,0:T(8,128)(2,1)S(1)} %get-tuple-element.4) | data formatting | bytes 2097152
  92.7 0.6 copy.16
